TPU v7x, 32 devices: a whole 2x2x4 slice. The times are simulated.
32 devices in a mesh: dp: 2 (over x), ctx: 16 (over z, y, core).
Axes of the slice: x: 2, y: 2, z: 4, core: 2. Of those that a mesh axis runs over, the one named last changes fastest.
Arguments:
- queries: bfloat16 [2, 8192, 1024], P('dp', 'ctx'), may hold values from -100 to 100
- key_states: bfloat16 [2, 8192, 128], P('dp', 'ctx'), may hold values from -4 to 4
- value_states: bfloat16 [2, 8192, 128], P('dp', 'ctx'), may hold values from -6 to 6
- doc_ids: int32 [2, 8192], P('dp', 'ctx'), may hold values from 0 to 7, never falling along the last dimension, each value on 1 to 3584 neighbouring positions
Outputs:
- attended: bfloat16 [2, 8192, 1024], P('dp', 'ctx')
Inputs may be any that keep to these rules, and one draw needn't show every extreme that they name: `doc_ids`: ids never fall along a sequence; each document spans 1 to 3584 tokens, and one document of each sequence spans exactly 3584.
All inputs are finite; a program needn't handle non-finite values.
Results may differ from a plain program's by a relative error of at most 0.0037.
Values may be sent and summed in bfloat16 or wider, within the bound.
No kernel may reach another device: no remote copies, remote signals or barrier semaphores. Data moves between devices by JAX's collectives and lax.ppermute only.
A program may use at most 64 MiB of HBM per device.

v0:
```python
import functools
import math

import jax
import jax.numpy as jnp
from jax import lax
from jax.experimental import pallas as pl
from jax.experimental.pallas import tpu as pltpu
from jax.sharding import PartitionSpec as P


ROWS = 256
META = 16
NEG = -1e30
KEYS = 256
AHEAD = 6
OWN_GROUP = 8
KEY_LIMIT = 4.0
CALM = 100.0
VMEM_LIMIT = 24 << 20


def pack_kernel(k_ref, v_ref, docs_ref, out_ref):
    tokens, size = k_ref.shape
    out_ref[:tokens, :size] = k_ref[...]
    for start in range(0, tokens, size):
        block = v_ref[start : start + size, :].astype(jnp.float32)
        out_ref[start : start + size, size:] = block.T.astype(jnp.bfloat16)
    width = 2 * size
    ids = (docs_ref[...] + 1).astype(jnp.float32)
    lines = [ids[:, i : i + width] for i in range(0, tokens, width)]
    lines.append(jnp.zeros((META - len(lines), width), jnp.float32))
    out_ref[tokens:, :] = jnp.concatenate(lines, axis=0).astype(jnp.bfloat16)


def pack(k, v, docs):
    tokens, size = k.shape
    return pl.pallas_call(
        pack_kernel,
        out_shape=jax.ShapeDtypeStruct((tokens + META, 2 * size), jnp.bfloat16),
        name="pack",
    )(k, v, docs)


def keys_twice(kv, start, count, size):
    k = kv[pl.ds(start, count), :size]
    return jnp.concatenate([k, k], axis=1)


def values_across(kv, start, count, size):
    blocks = [kv[pl.ds(start + i, size), size : 2 * size] for i in range(0, count, size)]
    return jnp.concatenate(blocks, axis=1)


def scores_of(keys, q):
    return lax.dot_general(
        keys, q, (((1,), (0,)), ((), ())), preferred_element_type=jnp.float32
    )


def folded(x, op):
    count, width = x.shape
    return op(x.reshape(count // 8, 8, width), axis=0)


def weigh(s, m, l_ref, acc_ref, at, values):
    count, width = s.shape
    p = jnp.exp2(s.reshape(count // 8, 8, width) - m)
    l_ref[at] += jnp.sum(p, axis=0)
    acc_ref[at] += jnp.dot(
        values, p.reshape(count, width).astype(jnp.bfloat16), preferred_element_type=jnp.float32
    )


def weigh_anew(s, m_ref, l_ref, acc_ref, at, values):
    old = m_ref[at]
    top = jnp.max(jnp.maximum(folded(s, jnp.max), old), axis=0, keepdims=True)
    fade = jnp.exp2(old - top)
    m_ref[at] = jnp.broadcast_to(top, old.shape)
    l_ref[at] *= fade
    acc_ref[at] *= fade[:1]
    weigh(s, m_ref[at], l_ref, acc_ref, at, values)


def pipelined(units):
    ahead = [scores() for scores, _ in units[:AHEAD]]
    for i, (_, rest) in enumerate(units):
        if i + AHEAD < len(units):
            ahead.append(units[i + AHEAD][0]())
        rest(ahead.pop(0))


def own_kernel(
    q_hbm, own_hbm, docs_hbm, qt_ref, m_ref, l_ref, acc_ref, facts_ref,
    q_ref, own_ref, docs_ref, bias_ref, kt_ref, sems,
):
    copies = [
        pltpu.make_async_copy(docs_hbm, docs_ref, sems.at[0]),
        pltpu.make_async_copy(own_hbm, own_ref, sems.at[1]),
        pltpu.make_async_copy(q_hbm, q_ref, sems.at[2]),
    ]
    for copy in copies:
        copy.start()
    tokens = q_ref.shape[0]
    heads, size = acc_ref.shape[0], acc_ref.shape[1]
    scale = size**-0.5 * math.log2(math.e)
    copies[0].wait()
    ids = docs_ref[...].astype(jnp.float32)
    ids_down = jnp.broadcast_to(ids, (size, tokens)).T
    ids_down = jnp.concatenate([ids_down] * (ROWS // size), axis=1)
    for row in range(0, tokens, ROWS):
        count = row + ROWS
        key = lax.broadcasted_iota(jnp.int32, (count, ROWS), 0)
        query = lax.broadcasted_iota(jnp.int32, (count, ROWS), 1) + row
        allowed = (ids_down[:count] == ids[:, row : row + ROWS]) & (key <= query)
        bias_ref[:count, row : row + ROWS] = jnp.where(allowed, 0.0, NEG)
    first = jnp.min(ids)
    facts_ref[0, 1] = first.astype(jnp.int32) + 1
    facts_ref[0, 2] = jnp.sum(jnp.where(ids == first, 1.0, 0.0)).astype(jnp.int32)
    l_ref[...] = jnp.zeros_like(l_ref)
    acc_ref[...] = jnp.zeros_like(acc_ref)
    copies[1].wait()
    kt_ref[...] = own_ref[:tokens, :size].T.astype(jnp.float32)
    copies[2].wait()

    def prepare(h, gap):
        col = pl.multiple_of(h * size, size)
        scaled = q_ref[:, pl.ds(col, size)].T.astype(jnp.float32) * scale
        high = scaled.astype(jnp.bfloat16)
        low = (scaled - high.astype(jnp.float32)).astype(jnp.bfloat16)
        qt_ref[h, :size, :] = high
        qt_ref[h, size:, :] = low
        own = jnp.sum(scaled * kt_ref[...], axis=0, keepdims=True)
        most = KEY_LIMIT * jnp.sum(jnp.abs(scaled), axis=0, keepdims=True)
        m_ref[h] = jnp.broadcast_to(own, (8, tokens))
        return jnp.maximum(gap, most - own)

    gap = jnp.zeros((1, tokens), jnp.float32)
    for h in range(heads):
        gap = prepare(h, gap)
    calm = jnp.max(gap) <= CALM
    facts_ref[0, 0] = calm.astype(jnp.int32)

    def units(h):
        made = []
        for row in range(0, tokens, ROWS):
            count = row + ROWS
            cols = slice(row, row + ROWS)

            def scores(count=count, cols=cols):
                s = scores_of(keys_twice(own_ref, 0, count, size), qt_ref[h, :, cols])
                return s + bias_ref[:count, cols]

            def rest(s, count=count, cols=cols):
                at, values = (h, slice(None), cols), values_across(own_ref, 0, count, size)
                weigh(s, m_ref[at], l_ref, acc_ref, at, values)

            def rest_anew(s, count=count, cols=cols):
                at, values = (h, slice(None), cols), values_across(own_ref, 0, count, size)
                weigh_anew(s, m_ref, l_ref, acc_ref, at, values)

            made.append((scores, rest, rest_anew))
        return made

    @pl.when(calm)
    def _():
        def body(i, carry):
            group = [u for g in range(OWN_GROUP) for u in units(OWN_GROUP * i + g)]
            pipelined([(scores, rest) for scores, rest, _ in group])
            return carry

        lax.fori_loop(0, heads // OWN_GROUP, body, 0)

    @pl.when(jnp.logical_not(calm))
    def _():
        def body(h, carry):
            pipelined([(scores, rest) for scores, _, rest in units(h)])
            return carry

        lax.fori_loop(0, heads, body, 0)


def own_part(q, own, docs, heads, size):
    tokens = q.shape[0]
    vmem = pl.BlockSpec(memory_space=pltpu.VMEM)
    q, own, docs = (pltpu.with_memory_space_constraint(x, pltpu.HBM) for x in (q, own, docs))
    return pl.pallas_call(
        own_kernel,
        out_shape=(
            jax.ShapeDtypeStruct((heads, 2 * size, tokens), jnp.bfloat16),
            jax.ShapeDtypeStruct((heads, 8, tokens), jnp.float32),
            jax.ShapeDtypeStruct((heads, 8, tokens), jnp.float32),
            jax.ShapeDtypeStruct((heads, size, tokens), jnp.float32),
            jax.ShapeDtypeStruct((1, 3), jnp.int32),
        ),
        in_specs=[pl.BlockSpec(memory_space=pltpu.HBM)] * 3,
        out_specs=(vmem, vmem, vmem, vmem, pl.BlockSpec(memory_space=pltpu.SMEM)),
        scratch_shapes=[
            pltpu.VMEM(q.shape, q.dtype),
            pltpu.VMEM(own.shape, own.dtype),
            pltpu.VMEM(docs.shape, docs.dtype),
            pltpu.VMEM((tokens, tokens), jnp.float32),
            pltpu.VMEM((size, tokens), jnp.float32),
            pltpu.SemaphoreType.DMA((3,)),
        ],
        compiler_params=pltpu.CompilerParams(vmem_limit_bytes=VMEM_LIMIT),
        name="own_part",
    )(q, own, docs)


def earlier_kernel(count, last, *refs):
    facts_ref, qt_ref = refs[:2]
    sources = refs[2 : 2 + count]
    m_in, l_in, acc_in = refs[2 + count : 5 + count]
    rest = refs[5 + count :]
    if last:
        out_hbm, m_ref, l_ref, acc_ref = rest[0], m_in, l_in, acc_in
        out_ref, out_sems = rest[-2:]
        rest = rest[1:-2]
    else:
        m_ref, l_ref, acc_ref = rest[:3]
        rest = rest[3:]
    kv_ref, bias_ref, valid_ref, sems = rest
    heads, size, tokens = acc_in.shape
    calm = facts_ref[0, 0] == 1
    first = facts_ref[0, 1].astype(jnp.float32)
    rows = facts_ref[0, 2]

    copies = [
        pltpu.make_async_copy(sources[j], kv_ref.at[j], sems.at[j]) for j in range(count)
    ]
    for copy in copies:
        copy.start()
    for copy in copies:
        copy.wait()
    found = [
        jnp.sum(jnp.where(kv_ref[j, tokens:, :].astype(jnp.float32) == first, 1.0, 0.0))
        for j in range(count)
    ]
    for j in range(count):
        valid_ref[j] = found[j].astype(jnp.int32)

    def unit(kv, h, row, start, keys, bias=None, anew=False):
        at = (h, slice(None), pl.ds(row, ROWS))

        def scores():
            s = scores_of(keys_twice(kv, start, keys, size), qt_ref[at])
            return s if bias is None else s + bias[pl.ds(start, keys), :]

        def rest(s):
            values = values_across(kv, start, keys, size)
            if anew:
                weigh_anew(s, m_ref, l_ref, acc_ref, at, values)
            else:
                query = lax.broadcasted_iota(jnp.int32, (8, ROWS), 1) + row
                m = jnp.where(query < rows, m_ref[at], -NEG)
                weigh(s, m, l_ref, acc_ref, at, values)

        return scores, rest

    def shard(j, carry):
        kv = kv_ref.at[j]
        valid = valid_ref[j]
        whole = calm & (valid == tokens)
        many = rows > tokens - ROWS

        def full(blocks):
            pipelined([
                unit(kv, h, row, start, KEYS)
                for h in range(heads)
                for row in blocks
                for start in range(0, tokens, KEYS)
            ])

        def blocks_of(work):
            def block(i, carry):
                work(pl.multiple_of(i * ROWS, ROWS))
                return carry

            lax.fori_loop(0, (rows + ROWS - 1) // ROWS, block, 0)

        @pl.when(whole & many)
        def _():
            full(range(0, tokens, ROWS))

        @pl.when(whole & jnp.logical_not(many))
        def _():
            blocks_of(lambda row: full([row]))

        def partly(anew, group):
            key = lax.broadcasted_iota(jnp.int32, (tokens, ROWS), 0)
            missing = jnp.where(key >= tokens - valid, 0.0, NEG)

            def work(row):
                query = lax.broadcasted_iota(jnp.int32, (8, ROWS), 1) + row
                if anew:
                    bias_ref[...] = jnp.where((query < rows)[:1], missing, NEG)
                else:
                    bias_ref[...] = missing

                def half(i, carry):
                    start = pl.multiple_of(i * ROWS, ROWS)

                    def some(g, carry):
                        pipelined([
                            unit(kv, group * g + h, row, start, ROWS, bias_ref, anew)
                            for h in range(group)
                        ])
                        return carry

                    if group == heads:
                        some(0, 0)
                    else:
                        lax.fori_loop(0, heads // group, some, 0)
                    return carry

                lax.fori_loop((tokens - valid) // ROWS, tokens // ROWS, half, 0)

            blocks_of(work)

        @pl.when((valid > 0) & calm & jnp.logical_not(whole))
        def _():
            partly(False, heads)

        @pl.when((valid > 0) & jnp.logical_not(calm))
        def _():
            partly(True, 1)

        return carry

    lax.fori_loop(0, count, shard, 0)

    if last:
        copies = []
        for h in range(heads):
            total = jnp.sum(l_ref[h], axis=0, keepdims=True)
            done = (acc_ref[h] * (1.0 / total)).astype(jnp.bfloat16)
            cols = slice(h * size, (h + 1) * size)
            out_ref[:, cols] = done.T
            copies.append(
                pltpu.make_async_copy(out_ref.at[:, cols], out_hbm.at[:, cols], out_sems.at[h])
            )
            copies[-1].start()
        for copy in copies:
            copy.wait()


def earlier_part(facts, qt, shards, state, last):
    heads, double, tokens = qt.shape
    size = double // 2
    count = len(shards)
    vmem = pl.BlockSpec(memory_space=pltpu.VMEM)
    hbm = pl.BlockSpec(memory_space=pltpu.HBM)
    scratch = [
        pltpu.VMEM((count,) + shards[0].shape, jnp.bfloat16),
        pltpu.VMEM((tokens, ROWS), jnp.float32),
        pltpu.SMEM((count,), jnp.int32),
        pltpu.SemaphoreType.DMA((count,)),
    ]
    if last:
        out_shape = jax.ShapeDtypeStruct((tokens, heads * size), jnp.bfloat16)
        out_specs = hbm
        aliases = {}
        scratch += [pltpu.VMEM(out_shape.shape, jnp.bfloat16), pltpu.SemaphoreType.DMA((heads,))]
    else:
        out_shape = tuple(jax.ShapeDtypeStruct(s.shape, s.dtype) for s in state)
        out_specs = (vmem,) * 3
        aliases = {2 + count + i: i for i in range(3)}
    return pl.pallas_call(
        functools.partial(earlier_kernel, count, last),
        out_shape=out_shape,
        in_specs=[pl.BlockSpec(memory_space=pltpu.SMEM), vmem] + [hbm] * count + [vmem] * 3,
        out_specs=out_specs,
        scratch_shapes=scratch,
        input_output_aliases=aliases,
        compiler_params=pltpu.CompilerParams(vmem_limit_bytes=VMEM_LIMIT),
        name="earlier_part_last" if last else "earlier_part",
    )(facts, qt, *shards, *state)


def send(x, by, which=None):
    length = lax.axis_size("ctx")
    pairs = [(i, i + by) for i in range(length - by) if which is None or i % 2 == which]
    return lax.ppermute(x, "ctx", pairs)


def swap(x):
    return lax.ppermute(x, "ctx", [(i, i ^ 1) for i in range(lax.axis_size("ctx"))])


def on_device(queries, key_states, value_states, doc_ids):
    size = key_states.shape[2]
    heads = queries.shape[2] // size
    own = pack(key_states[0], value_states[0], doc_ids)
    four = send(own, 4)
    two = send(own, 2)
    one = send(own, 1, 0)
    qt, *state, facts = own_part(queries[0], own, doc_ids, heads, size)
    four, facts = lax.optimization_barrier((four, facts))
    six = send(four, 2)
    seven = send(four, 3, 1)
    swapped_four = swap(four)
    swapped_two = swap(two)
    early = [one, four, swapped_four, two, swapped_two]
    state = earlier_part(facts, qt, early, state, False)
    six, state = lax.optimization_barrier((six, state))
    swapped_six = swap(six)
    out = earlier_part(facts, qt, [six, seven, swapped_six], state, True)
    return out[None]


def solution(mesh):
    in_specs = (P("dp", "ctx", None), P("dp", "ctx", None), P("dp", "ctx", None), P("dp", "ctx"))
    out_specs = P("dp", "ctx", None)
    return jax.shard_map(
        on_device, mesh=mesh, in_specs=in_specs, out_specs=out_specs, check_vma=False
    )
```

profile of v0, /device:TPU:12, one launch (start us, length us, event | category | flops | bytes accessed | tf_op | source)
XLA Modules:
  0.0 115.2 jit_solution(4694463554802406484)
XLA Ops:
  0.0 1.8 %pack.1.own_hbm = bf16[528,256]{1,0:T(8,128)(2,1)} custom-call(bf16[512,128]{1,0:T(8,128)(2,1)} %bitcast.5, bf16[512,128]{1,0:T(8,128)(2,1)} %bitcast.6, s32[1,512]{1,0:T(1,128)} %docs_hbm.1), custom_call_target="tpu_custom_call" | custom-call | tf_op jit(solution)/shard_map/pack/pallas_call | solution.py:38
  1.8 3.5 %collective-permute-start = (bf16[528,256]{1,0:T(8,128)(2,1)}, bf16[528,256]{1,0:T(8,128)(2,1)S(1)}, u32[]{:S(2)}, u32[]{:S(2)}) collective-permute-start(bf16[528,256]{1,0:T(8,128)(2,1)} %pack.1.own_hbm), channel_id=1, source_target_pairs={{0,4},{1,5},{2,6},{3,7},{4,8},{5,9},{6,10},{7,11},{8,12},{9,13},{1... | collective-permute-start | bytes 811016 | tf_op jit(solution)/shard_map/ppermute | solution.py:384
  5.3 3.4 %collective-permute-start.4 = (bf16[528,256]{1,0:T(8,128)(2,1)}, bf16[528,256]{1,0:T(8,128)(2,1)S(1)}, u32[]{:S(2)}, u32[]{:S(2)}) collective-permute-start(bf16[528,256]{1,0:T(8,128)(2,1)} %pack.1.own_hbm), channel_id=1, source_target_pairs={{0,2},{1,3},{2,4},{3,5},{4,6},{5,7},{6,8},{7,9},{8,10},{9,11},{10,... | collective-permute-start | bytes 811016 | tf_op jit(solution)/shard_map/ppermute | solution.py:384
  8.7 1.3 %collective-permute-start.2 = (bf16[528,256]{1,0:T(8,128)(2,1)}, bf16[528,256]{1,0:T(8,128)(2,1)S(1)}, u32[]{:S(2)}, u32[]{:S(2)}) collective-permute-start(bf16[528,256]{1,0:T(8,128)(2,1)} %pack.1.own_hbm), channel_id=1, source_target_pairs={{0,1},{2,3},{4,5},{6,7},{8,9},{10,11},{12,13},{14,15},{16,17},{18,... | collective-permute-start | bytes 811016 | tf_op jit(solution)/shard_map/ppermute | solution.py:384
  10.0 7.3 %own_part.1 = (bf16[8,256,512]{2,1,0:T(8,128)(2,1)S(1)}, f32[8,8,512]{2,1,0:T(8,128)S(1)}, f32[8,8,512]{2,1,0:T(8,128)S(1)}, f32[8,128,512]{2,1,0:T(8,128)S(1)}, s32[1,3]{1,0:T(1,128)S(1)}) custom-call(bf16[512,1024]{1,0:T(8,128)(2,1)} %bitcast.4, bf16[528,256]{1,0:T(8,128)(2,1)} %pack.1.own_hbm, s32[1,512]{1,0:T(1,128)} %docs_hbm.1), custom_call_target="tpu_custom_call" | custom-call | tf_op jit(solution)/shard_map/own_part/pallas_call | solution.py:187
  17.3 0.0 collective-permute-done.refs_3_
  17.4 0.1 collective-permute-start.3
  17.4 0.0 collective-permute-done.4.refs_5_
  17.4 0.5 collective-permute-start.5
  17.9 4.3 %collective-permute-start.1 = (bf16[528,256]{1,0:T(8,128)(2,1)S(1)}, bf16[528,256]{1,0:T(8,128)(2,1)S(1)}, u32[]{:S(2)}, u32[]{:S(2)}) collective-permute-start(bf16[528,256]{1,0:T(8,128)(2,1)S(1)} %collective-permute-done.refs_3_), channel_id=1, source_target_pairs={{0,2},{1,3},{2,4},{3,5},{4,6},{5,7},{6,8},{7,9},{8,10},{9,11},{10,... | collective-permute-start | bytes 811016 | tf_op jit(solution)/shard_map/ppermute | solution.py:384
  22.3 1.5 %collective-permute-start.6 = (bf16[528,256]{1,0:T(8,128)(2,1)S(1)}, bf16[528,256]{1,0:T(8,128)(2,1)S(1)}, u32[]{:S(2)}, u32[]{:S(2)}) collective-permute-start(bf16[528,256]{1,0:T(8,128)(2,1)S(1)} %collective-permute-done.refs_3_), channel_id=1, source_target_pairs={{1,4},{3,6},{5,8},{7,10},{9,12},{11,14},{17,20},{19,22},{21,24},{2... | collective-permute-start | bytes 811016 | tf_op jit(solution)/shard_map/ppermute | solution.py:384
  23.8 0.0 collective-permute-done.2.refs_2_
  23.8 0.0 collective-permute-done.3.refs_4_
  23.8 0.0 collective-permute-done.5.refs_6_
  23.8 57.4 %earlier_part.1 = (f32[8,8,512]{2,1,0:T(8,128)S(1)}, f32[8,8,512]{2,1,0:T(8,128)S(1)}, f32[8,128,512]{2,1,0:T(8,128)S(1)}) custom-call(s32[1,3]{1,0:T(1,128)S(1)} %get-tuple-element.20.refs_0_, bf16[8,256,512]{2,1,0:T(8,128)(2,1)S(1)} %get-tuple-element.21.refs_1_, ...), custom_call_target="tpu_custom_call", output_to_operand_aliasing={{0}: (7, {}), {1}: (8, {}), {2}: (9, {})} | custom-call | tf_op jit(solution)/shard_map/earlier_part/pallas_call | solution.py:369
  81.2 0.0 collective-permute-done.1.refs_2_
  81.2 16.5 %collective-permute-start.7 = (bf16[528,256]{1,0:T(8,128)(2,1)S(1)}, bf16[528,256]{1,0:T(8,128)(2,1)S(1)}, u32[]{:S(2)}, u32[]{:S(2)}) collective-permute-start(bf16[528,256]{1,0:T(8,128)(2,1)S(1)} %collective-permute-done.1.refs_2_), channel_id=1, source_target_pairs={{0,1},{1,0},{2,3},{3,2},{4,5},{5,4},{6,7},{7,6},{8,9},{9,8},{10,11... | collective-permute-start | bytes 811016 | tf_op jit(solution)/shard_map/ppermute | solution.py:388
  97.7 0.0 collective-permute-done.6.refs_3_
  97.7 1.2 %collective-permute-done.7.refs_4_ = bf16[528,256]{1,0:T(8,128)(2,1)S(1)} collective-permute-done((bf16[528,256]{1,0:T(8,128)(2,1)S(1)}, bf16[528,256]{1,0:T(8,128)(2,1)S(1)}, u32[]{:S(2)}, u32[]{:S(2)}) %collective-permute-start.7) | collective-permute-done | bytes 270368 | tf_op jit(solution)/shard_map/ppermute | solution.py:388
  98.9 16.1 %earlier_part_last.1 = bf16[512,1024]{1,0:T(8,128)(2,1)} custom-call(s32[1,3]{1,0:T(1,128)S(1)} %get-tuple-element.20.refs_0_, bf16[8,256,512]{2,1,0:T(8,128)(2,1)S(1)} %get-tuple-element.21.refs_1_, bf16[528,256]{1,0:T(8,128)(2,1)S(1)} %collective-permute-done.1.refs_2_, bf16[528,256]{1,0:T(8,128)(2,1)S(1)} %collective-permute-done.6.refs_3_, ...), custom_call_target="tpu_custom_call" | custom-call | tf_op jit(solution)/shard_map/earlier_part_last/pallas_call | solution.py:369
Async XLA Ops:
  1.8 15.6 %collective-permute-start = (bf16[528,256]{1,0:T(8,128)(2,1)}, bf16[528,256]{1,0:T(8,128)(2,1)S(1)}, u32[]{:S(2)}, u32[]{:S(2)}) collective-permute-start(bf16[528,256]{1,0:T(8,128)(2,1)} %pack.1.own_hbm), channel_id=1, source_target_pairs={{0,4},{1,5},{2,6},{3,7},{4,8},{5,9},{6,10},{7,11},{8,12},{9,13},{1... | collective-permute-start | bytes 811016 | tf_op jit(solution)/shard_map/ppermute | solution.py:384
  5.3 12.2 %collective-permute-start.4 = (bf16[528,256]{1,0:T(8,128)(2,1)}, bf16[528,256]{1,0:T(8,128)(2,1)S(1)}, u32[]{:S(2)}, u32[]{:S(2)}) collective-permute-start(bf16[528,256]{1,0:T(8,128)(2,1)} %pack.1.own_hbm), channel_id=1, source_target_pairs={{0,2},{1,3},{2,4},{3,5},{4,6},{5,7},{6,8},{7,9},{8,10},{9,11},{10,... | collective-permute-start | bytes 811016 | tf_op jit(solution)/shard_map/ppermute | solution.py:384
  8.7 15.1 %collective-permute-start.2 = (bf16[528,256]{1,0:T(8,128)(2,1)}, bf16[528,256]{1,0:T(8,128)(2,1)S(1)}, u32[]{:S(2)}, u32[]{:S(2)}) collective-permute-start(bf16[528,256]{1,0:T(8,128)(2,1)} %pack.1.own_hbm), channel_id=1, source_target_pairs={{0,1},{2,3},{4,5},{6,7},{8,9},{10,11},{12,13},{14,15},{16,17},{18,... | collective-permute-start | bytes 811016 | tf_op jit(solution)/shard_map/ppermute | solution.py:384
  17.4 6.4 %collective-permute-start.3 = (bf16[528,256]{1,0:T(8,128)(2,1)S(1)}, bf16[528,256]{1,0:T(8,128)(2,1)S(1)}, u32[]{:S(2)}, u32[]{:S(2)}) collective-permute-start(bf16[528,256]{1,0:T(8,128)(2,1)S(1)} %collective-permute-done.refs_3_), channel_id=1, source_target_pairs={{0,1},{1,0},{2,3},{3,2},{4,5},{5,4},{6,7},{7,6},{8,9},{9,8},{10,11... | collective-permute-start | bytes 811016 | tf_op jit(solution)/shard_map/ppermute | solution.py:388
  17.4 6.3 %collective-permute-start.5 = (bf16[528,256]{1,0:T(8,128)(2,1)S(1)}, bf16[528,256]{1,0:T(8,128)(2,1)S(1)}, u32[]{:S(2)}, u32[]{:S(2)}) collective-permute-start(bf16[528,256]{1,0:T(8,128)(2,1)S(1)} %collective-permute-done.4.refs_5_), channel_id=1, source_target_pairs={{0,1},{1,0},{2,3},{3,2},{4,5},{5,4},{6,7},{7,6},{8,9},{9,8},{10,11... | collective-permute-start | bytes 811016 | tf_op jit(solution)/shard_map/ppermute | solution.py:388
  17.9 63.3 %collective-permute-start.1 = (bf16[528,256]{1,0:T(8,128)(2,1)S(1)}, bf16[528,256]{1,0:T(8,128)(2,1)S(1)}, u32[]{:S(2)}, u32[]{:S(2)}) collective-permute-start(bf16[528,256]{1,0:T(8,128)(2,1)S(1)} %collective-permute-done.refs_3_), channel_id=1, source_target_pairs={{0,2},{1,3},{2,4},{3,5},{4,6},{5,7},{6,8},{7,9},{8,10},{9,11},{10,... | collective-permute-start | bytes 811016 | tf_op jit(solution)/shard_map/ppermute | solution.py:384
  22.3 75.4 %collective-permute-start.6 = (bf16[528,256]{1,0:T(8,128)(2,1)S(1)}, bf16[528,256]{1,0:T(8,128)(2,1)S(1)}, u32[]{:S(2)}, u32[]{:S(2)}) collective-permute-start(bf16[528,256]{1,0:T(8,128)(2,1)S(1)} %collective-permute-done.refs_3_), channel_id=1, source_target_pairs={{1,4},{3,6},{5,8},{7,10},{9,12},{11,14},{17,20},{19,22},{21,24},{2... | collective-permute-start | bytes 811016 | tf_op jit(solution)/shard_map/ppermute | solution.py:384
  81.2 17.7 %collective-permute-start.7 = (bf16[528,256]{1,0:T(8,128)(2,1)S(1)}, bf16[528,256]{1,0:T(8,128)(2,1)S(1)}, u32[]{:S(2)}, u32[]{:S(2)}) collective-permute-start(bf16[528,256]{1,0:T(8,128)(2,1)S(1)} %collective-permute-done.1.refs_2_), channel_id=1, source_target_pairs={{0,1},{1,0},{2,3},{3,2},{4,5},{5,4},{6,7},{7,6},{8,9},{9,8},{10,11... | collective-permute-start | bytes 811016 | tf_op jit(solution)/shard_map/ppermute | solution.py:388
where the time goes:
time: 116 us; the launch traced here: 115 us
  Pallas kernels  82.6 us (71%)
  starting transfers between devices  31.1 us (27%)
  waiting for transfers between devices  1.19 us (1%)
    pallas_call x2, Pallas kernels, earlier_part(): pl.pallas_call(functools.partial(earlier_kernel, count, last), out_shape=...  73.5 us
    ppermute x3, starting transfers between devices, swap(): lax.ppermute(x, 'ctx', [(i, i ^ 1) for i in range(lax.axis_size('ctx'))])  17.1 us
    ppermute x5, starting transfers between devices, send(): return lax.ppermute(x, 'ctx', pairs)  14 us
    pallas_call x1, Pallas kernels, own_part(): pl.pallas_call(own_kernel, out_shape=(jax.ShapeDtypeStruct((heads, 2 * si...  7.33 us
  transfers between devices with their start and end apart: 8, of which 1 were waited for; matrix products, arithmetic and copies ran while one was open for 0% of the time, Pallas kernels for 56%

commit v1 on v0

--- a/solution.py
+++ b/solution.py
@@ -20,7 +20,16 @@
 VMEM_LIMIT = 24 << 20
 
 
-def pack_kernel(k_ref, v_ref, docs_ref, out_ref):
+def pack_kernel(*refs):
+    sources, (q_ref, out_ref), (k_ref, v_ref, docs_ref, sems) = refs[:4], refs[4:6], refs[6:]
+    fetches = [
+        pltpu.make_async_copy(source, target, sems.at[i])
+        for i, (source, target) in enumerate(zip(sources, (q_ref, k_ref, v_ref, docs_ref)))
+    ]
+    for fetch in fetches[1:] + fetches[:1]:
+        fetch.start()
+    for fetch in fetches[1:]:
+        fetch.wait()
     tokens, size = k_ref.shape
     out_ref[:tokens, :size] = k_ref[...]
     for start in range(0, tokens, size):
@@ -31,15 +40,30 @@
     lines = [ids[:, i : i + width] for i in range(0, tokens, width)]
     lines.append(jnp.zeros((META - len(lines), width), jnp.float32))
     out_ref[tokens:, :] = jnp.concatenate(lines, axis=0).astype(jnp.bfloat16)
-
-
-def pack(k, v, docs):
+    fetches[0].wait()
+
+
+def pack(q, k, v, docs):
     tokens, size = k.shape
+    vmem = pl.BlockSpec(memory_space=pltpu.VMEM)
+    arrays = [pltpu.with_memory_space_constraint(x, pltpu.HBM) for x in (q, k, v, docs)]
     return pl.pallas_call(
         pack_kernel,
-        out_shape=jax.ShapeDtypeStruct((tokens + META, 2 * size), jnp.bfloat16),
+        out_shape=(
+            pltpu.VMEM(q.shape, q.dtype),
+            pltpu.VMEM((tokens + META, 2 * size), jnp.bfloat16),
+        ),
+        in_specs=[pl.BlockSpec(memory_space=pltpu.HBM)] * 4,
+        out_specs=(vmem, vmem),
+        scratch_shapes=[
+            pltpu.VMEM(k.shape, k.dtype),
+            pltpu.VMEM(v.shape, v.dtype),
+            pltpu.VMEM(docs.shape, docs.dtype),
+            pltpu.SemaphoreType.DMA((4,)),
+        ],
+        compiler_params=pltpu.CompilerParams(vmem_limit_bytes=VMEM_LIMIT),
         name="pack",
-    )(k, v, docs)
+    )(*arrays)
 
 
 def keys_twice(kv, start, count, size):
@@ -91,21 +115,13 @@
 
 
 def own_kernel(
-    q_hbm, own_hbm, docs_hbm, qt_ref, m_ref, l_ref, acc_ref, facts_ref,
-    q_ref, own_ref, docs_ref, bias_ref, kt_ref, sems,
+    q_ref, own_ref, qt_ref, m_ref, l_ref, acc_ref, facts_ref, bias_ref, kt_ref
 ):
-    copies = [
-        pltpu.make_async_copy(docs_hbm, docs_ref, sems.at[0]),
-        pltpu.make_async_copy(own_hbm, own_ref, sems.at[1]),
-        pltpu.make_async_copy(q_hbm, q_ref, sems.at[2]),
-    ]
-    for copy in copies:
-        copy.start()
     tokens = q_ref.shape[0]
     heads, size = acc_ref.shape[0], acc_ref.shape[1]
     scale = size**-0.5 * math.log2(math.e)
-    copies[0].wait()
-    ids = docs_ref[...].astype(jnp.float32)
+    lines = own_ref[tokens:, :].astype(jnp.float32)
+    ids = jnp.concatenate([lines[i : i + 1] for i in range(tokens // (2 * size))], axis=1)
     ids_down = jnp.broadcast_to(ids, (size, tokens)).T
     ids_down = jnp.concatenate([ids_down] * (ROWS // size), axis=1)
     for row in range(0, tokens, ROWS):
@@ -115,13 +131,11 @@
         allowed = (ids_down[:count] == ids[:, row : row + ROWS]) & (key <= query)
         bias_ref[:count, row : row + ROWS] = jnp.where(allowed, 0.0, NEG)
     first = jnp.min(ids)
-    facts_ref[0, 1] = first.astype(jnp.int32) + 1
+    facts_ref[0, 1] = first.astype(jnp.int32)
     facts_ref[0, 2] = jnp.sum(jnp.where(ids == first, 1.0, 0.0)).astype(jnp.int32)
     l_ref[...] = jnp.zeros_like(l_ref)
     acc_ref[...] = jnp.zeros_like(acc_ref)
-    copies[1].wait()
     kt_ref[...] = own_ref[:tokens, :size].T.astype(jnp.float32)
-    copies[2].wait()
 
     def prepare(h, gap):
         col = pl.multiple_of(h * size, size)
@@ -180,10 +194,9 @@
         lax.fori_loop(0, heads, body, 0)
 
 
-def own_part(q, own, docs, heads, size):
+def own_part(q, own, heads, size):
     tokens = q.shape[0]
     vmem = pl.BlockSpec(memory_space=pltpu.VMEM)
-    q, own, docs = (pltpu.with_memory_space_constraint(x, pltpu.HBM) for x in (q, own, docs))
     return pl.pallas_call(
         own_kernel,
         out_shape=(
@@ -193,19 +206,15 @@
             jax.ShapeDtypeStruct((heads, size, tokens), jnp.float32),
             jax.ShapeDtypeStruct((1, 3), jnp.int32),
         ),
-        in_specs=[pl.BlockSpec(memory_space=pltpu.HBM)] * 3,
+        in_specs=[vmem, vmem],
         out_specs=(vmem, vmem, vmem, vmem, pl.BlockSpec(memory_space=pltpu.SMEM)),
         scratch_shapes=[
-            pltpu.VMEM(q.shape, q.dtype),
-            pltpu.VMEM(own.shape, own.dtype),
-            pltpu.VMEM(docs.shape, docs.dtype),
             pltpu.VMEM((tokens, tokens), jnp.float32),
             pltpu.VMEM((size, tokens), jnp.float32),
-            pltpu.SemaphoreType.DMA((3,)),
         ],
         compiler_params=pltpu.CompilerParams(vmem_limit_bytes=VMEM_LIMIT),
         name="own_part",
-    )(q, own, docs)
+    )(q, own)
 
 
 def earlier_kernel(count, last, *refs):
@@ -220,21 +229,16 @@
     else:
         m_ref, l_ref, acc_ref = rest[:3]
         rest = rest[3:]
-    kv_ref, bias_ref, valid_ref, sems = rest
+    kv_ref, bias_ref, valid_ref = rest
     heads, size, tokens = acc_in.shape
     calm = facts_ref[0, 0] == 1
     first = facts_ref[0, 1].astype(jnp.float32)
     rows = facts_ref[0, 2]
 
-    copies = [
-        pltpu.make_async_copy(sources[j], kv_ref.at[j], sems.at[j]) for j in range(count)
-    ]
-    for copy in copies:
-        copy.start()
-    for copy in copies:
-        copy.wait()
+    for j in range(count):
+        kv_ref[j] = sources[j][...]
     found = [
-        jnp.sum(jnp.where(kv_ref[j, tokens:, :].astype(jnp.float32) == first, 1.0, 0.0))
+        jnp.sum(jnp.where(sources[j][tokens:, :].astype(jnp.float32) == first, 1.0, 0.0))
         for j in range(count)
     ]
     for j in range(count):
@@ -355,7 +359,6 @@
         pltpu.VMEM((count,) + shards[0].shape, jnp.bfloat16),
         pltpu.VMEM((tokens, ROWS), jnp.float32),
         pltpu.SMEM((count,), jnp.int32),
-        pltpu.SemaphoreType.DMA((count,)),
     ]
     if last:
         out_shape = jax.ShapeDtypeStruct((tokens, heads * size), jnp.bfloat16)
@@ -369,7 +372,7 @@
     return pl.pallas_call(
         functools.partial(earlier_kernel, count, last),
         out_shape=out_shape,
-        in_specs=[pl.BlockSpec(memory_space=pltpu.SMEM), vmem] + [hbm] * count + [vmem] * 3,
+        in_specs=[pl.BlockSpec(memory_space=pltpu.SMEM)] + [vmem] * (count + 4),
         out_specs=out_specs,
         scratch_shapes=scratch,
         input_output_aliases=aliases,
@@ -391,21 +394,21 @@
 def on_device(queries, key_states, value_states, doc_ids):
     size = key_states.shape[2]
     heads = queries.shape[2] // size
-    own = pack(key_states[0], value_states[0], doc_ids)
+    q, own = pack(queries[0], key_states[0], value_states[0], doc_ids)
     four = send(own, 4)
     two = send(own, 2)
     one = send(own, 1, 0)
-    qt, *state, facts = own_part(queries[0], own, doc_ids, heads, size)
+    qt, *state, facts = own_part(q, own, heads, size)
     four, facts = lax.optimization_barrier((four, facts))
     six = send(four, 2)
     seven = send(four, 3, 1)
     swapped_four = swap(four)
     swapped_two = swap(two)
-    early = [one, four, swapped_four, two, swapped_two]
-    state = earlier_part(facts, qt, early, state, False)
-    six, state = lax.optimization_barrier((six, state))
+    state = earlier_part(facts, qt, [one, four, swapped_four, two], state, False)
+    six, swapped_two, state = lax.optimization_barrier((six, swapped_two, state))
     swapped_six = swap(six)
-    out = earlier_part(facts, qt, [six, seven, swapped_six], state, True)
+    state = earlier_part(facts, qt, [swapped_two, seven], state, False)
+    out = earlier_part(facts, qt, [six, swapped_six], state, True)
     return out[None]
 
 

time: 116 us -> 111 us (0.957)
  starting transfers between devices: 31.1 us -> 27.9 us
  waiting for transfers between devices: 1.19 us -> 0.02 us
    ppermute x3, starting transfers between devices: 17.1 us -> 14.8 us  [swap(): lax.ppermute(x, 'ctx', [(i, i ^ 1) for i in range(lax.axis_size('ctx'))])]
    ppermute x3, waiting for transfers between devices: 1.18 us -> 0.01 us  [swap(): lax.ppermute(x, 'ctx', [(i, i ^ 1) for i in range(lax.axis_size('ctx'))])]
    pallas_call x2 -> x3, Pallas kernels: 73.5 us -> 74 us  [earlier_part(): pl.pallas_call(functools.partial(earlier_kernel, count, last), out_shape=...]
  transfers between devices with their start and end apart: 8 -> 8, of which waited for: 1 -> 0; matrix products, arithmetic and copies ran while one was open for 0% -> 0% of each run, Pallas kernels for 56% -> 58%
where the time goes in v1:
time: 111 us; the launch traced here: 110 us
  Pallas kernels  81.7 us (74%)
  starting transfers between devices  27.9 us (25%)
    pallas_call x3, Pallas kernels, earlier_part(): pl.pallas_call(functools.partial(earlier_kernel, count, last), out_shape=...  74 us
    ppermute x3, starting transfers between devices, swap(): lax.ppermute(x, 'ctx', [(i, i ^ 1) for i in range(lax.axis_size('ctx'))])  14.8 us
    ppermute x5, starting transfers between devices, send(): return lax.ppermute(x, 'ctx', pairs)  13.1 us
    pallas_call x1, Pallas kernels, own_part(): pl.pallas_call(own_kernel, out_shape=(jax.ShapeDtypeStruct((heads, 2 * si...  6.26 us
  transfers between devices with their start and end apart: 8, of which 0 were waited for; matrix products, arithmetic and copies ran while one was open for 0% of the time, Pallas kernels for 58%

profile of v1, /device:TPU:12, one launch (start us, length us, event | category | flops | bytes accessed | tf_op | source)
XLA Modules:
  0.0 110.0 jit_solution(1331134164991146307)
XLA Ops:
  0.0 1.4 %pack.1 = (bf16[512,1024]{1,0:T(8,128)(2,1)S(1)}, bf16[528,256]{1,0:T(8,128)(2,1)S(1)}) custom-call(bf16[512,1024]{1,0:T(8,128)(2,1)} %bitcast.4, bf16[512,128]{1,0:T(8,128)(2,1)} %bitcast.5, bf16[512,128]{1,0:T(8,128)(2,1)} %bitcast.6, s32[1,512]{1,0:T(1,128)} %refs_3_.1), custom_call_target="tpu_custom_call" | custom-call | tf_op jit(solution)/shard_map/pack/pallas_call | solution.py:50
  1.4 3.5 %collective-permute-start = (bf16[528,256]{1,0:T(8,128)(2,1)S(1)}, bf16[528,256]{1,0:T(8,128)(2,1)S(1)}, u32[]{:S(2)}, u32[]{:S(2)}) collective-permute-start(bf16[528,256]{1,0:T(8,128)(2,1)S(1)} %get-tuple-element.25.own_ref), channel_id=1, source_target_pairs={{0,4},{1,5},{2,6},{3,7},{4,8},{5,9},{6,10},{7,11},{8,12},{9,13},{1... | collective-permute-start | bytes 811016 | tf_op jit(solution)/shard_map/ppermute | solution.py:387
  4.9 3.4 %collective-permute-start.2 = (bf16[528,256]{1,0:T(8,128)(2,1)S(1)}, bf16[528,256]{1,0:T(8,128)(2,1)S(1)}, u32[]{:S(2)}, u32[]{:S(2)}) collective-permute-start(bf16[528,256]{1,0:T(8,128)(2,1)S(1)} %get-tuple-element.25.own_ref), channel_id=1, source_target_pairs={{0,2},{1,3},{2,4},{3,5},{4,6},{5,7},{6,8},{7,9},{8,10},{9,11},{10,... | collective-permute-start | bytes 811016 | tf_op jit(solution)/shard_map/ppermute | solution.py:387
  8.4 1.3 %collective-permute-start.4 = (bf16[528,256]{1,0:T(8,128)(2,1)S(1)}, bf16[528,256]{1,0:T(8,128)(2,1)S(1)}, u32[]{:S(2)}, u32[]{:S(2)}) collective-permute-start(bf16[528,256]{1,0:T(8,128)(2,1)S(1)} %get-tuple-element.25.own_ref), channel_id=1, source_target_pairs={{0,1},{2,3},{4,5},{6,7},{8,9},{10,11},{12,13},{14,15},{16,17},{18,... | collective-permute-start | bytes 811016 | tf_op jit(solution)/shard_map/ppermute | solution.py:387
  9.7 6.3 %own_part.1 = (bf16[8,256,512]{2,1,0:T(8,128)(2,1)S(1)}, f32[8,8,512]{2,1,0:T(8,128)S(1)}, f32[8,8,512]{2,1,0:T(8,128)S(1)}, f32[8,128,512]{2,1,0:T(8,128)S(1)}, s32[1,3]{1,0:T(1,128)S(1)}) custom-call(bf16[512,1024]{1,0:T(8,128)(2,1)S(1)} %get-tuple-element.26.q_ref, bf16[528,256]{1,0:T(8,128)(2,1)S(1)} %get-tuple-element.25.own_ref), custom_call_target="tpu_custom_call" | custom-call | tf_op jit(solution)/shard_map/own_part/pallas_call | solution.py:200
  15.9 0.0 collective-permute-done.refs_3_
  15.9 0.1 collective-permute-start.5
  16.0 3.4 %collective-permute-start.1 = (bf16[528,256]{1,0:T(8,128)(2,1)S(1)}, bf16[528,256]{1,0:T(8,128)(2,1)S(1)}, u32[]{:S(2)}, u32[]{:S(2)}) collective-permute-start(bf16[528,256]{1,0:T(8,128)(2,1)S(1)} %collective-permute-done.refs_3_), channel_id=1, source_target_pairs={{0,2},{1,3},{2,4},{3,5},{4,6},{5,7},{6,8},{7,9},{8,10},{9,11},{10,... | collective-permute-start | bytes 811016 | tf_op jit(solution)/shard_map/ppermute | solution.py:387
  19.5 0.0 collective-permute-done.2.refs_5_
  19.5 0.3 collective-permute-start.3
  19.7 1.5 %collective-permute-start.7 = (bf16[528,256]{1,0:T(8,128)(2,1)S(1)}, bf16[528,256]{1,0:T(8,128)(2,1)S(1)}, u32[]{:S(2)}, u32[]{:S(2)}) collective-permute-start(bf16[528,256]{1,0:T(8,128)(2,1)S(1)} %collective-permute-done.refs_3_), channel_id=1, source_target_pairs={{1,4},{3,6},{5,8},{7,10},{9,12},{11,14},{17,20},{19,22},{21,24},{2... | collective-permute-start | bytes 811016 | tf_op jit(solution)/shard_map/ppermute | solution.py:387
  21.2 0.0 collective-permute-done.4.refs_2_
  21.2 0.0 collective-permute-done.5.refs_4_
  21.2 43.2 %earlier_part.2 = (f32[8,8,512]{2,1,0:T(8,128)S(1)}, f32[8,8,512]{2,1,0:T(8,128)S(1)}, f32[8,128,512]{2,1,0:T(8,128)S(1)}) custom-call(s32[1,3]{1,0:T(1,128)S(1)} %get-tuple-element.28.refs_0_, bf16[8,256,512]{2,1,0:T(8,128)(2,1)S(1)} %get-tuple-element.29.refs_1_, ...), custom_call_target="tpu_custom_call", output_to_operand_aliasing={{0}: (6, {}), {1}: (7, {}), {2}: (8, {})} | custom-call | tf_op jit(solution)/shard_map/earlier_part/pallas_call | solution.py:372
  64.4 0.0 collective-permute-done.1.refs_2_
  64.4 0.0 collective-permute-done.3.refs_2_
  64.5 14.5 %collective-permute-start.6 = (bf16[528,256]{1,0:T(8,128)(2,1)S(1)}, bf16[528,256]{1,0:T(8,128)(2,1)S(1)}, u32[]{:S(2)}, u32[]{:S(2)}) collective-permute-start(bf16[528,256]{1,0:T(8,128)(2,1)S(1)} %collective-permute-done.1.refs_2_), channel_id=1, source_target_pairs={{0,1},{1,0},{2,3},{3,2},{4,5},{5,4},{6,7},{7,6},{8,9},{9,8},{10,11... | collective-permute-start | bytes 811016 | tf_op jit(solution)/shard_map/ppermute | solution.py:391
  78.9 0.0 collective-permute-done.7.refs_3_
  78.9 14.8 %earlier_part.3 = (f32[8,8,512]{2,1,0:T(8,128)S(1)}, f32[8,8,512]{2,1,0:T(8,128)S(1)}, f32[8,128,512]{2,1,0:T(8,128)S(1)}) custom-call(s32[1,3]{1,0:T(1,128)S(1)} %get-tuple-element.28.refs_0_, bf16[8,256,512]{2,1,0:T(8,128)(2,1)S(1)} %get-tuple-element.29.refs_1_, ...), custom_call_target="tpu_custom_call", output_to_operand_aliasing={{0}: (4, {}), {1}: (5, {}), {2}: (6, {})} | custom-call | tf_op jit(solution)/shard_map/earlier_part/pallas_call | solution.py:372
  93.8 0.0 collective-permute-done.6.refs_3_
  93.8 16.0 %earlier_part_last.1 = bf16[512,1024]{1,0:T(8,128)(2,1)} custom-call(s32[1,3]{1,0:T(1,128)S(1)} %get-tuple-element.28.refs_0_, bf16[8,256,512]{2,1,0:T(8,128)(2,1)S(1)} %get-tuple-element.29.refs_1_, bf16[528,256]{1,0:T(8,128)(2,1)S(1)} %collective-permute-done.1.refs_2_, bf16[528,256]{1,0:T(8,128)(2,1)S(1)} %collective-permute-done.6.refs_3_, ...), custom_call_target="tpu_custom_call" | custom-call | tf_op jit(solution)/shard_map/earlier_part_last/pallas_call | solution.py:372
Async XLA Ops:
  1.4 14.5 %collective-permute-start = (bf16[528,256]{1,0:T(8,128)(2,1)S(1)}, bf16[528,256]{1,0:T(8,128)(2,1)S(1)}, u32[]{:S(2)}, u32[]{:S(2)}) collective-permute-start(bf16[528,256]{1,0:T(8,128)(2,1)S(1)} %get-tuple-element.25.own_ref), channel_id=1, source_target_pairs={{0,4},{1,5},{2,6},{3,7},{4,8},{5,9},{6,10},{7,11},{8,12},{9,13},{1... | collective-permute-start | bytes 811016 | tf_op jit(solution)/shard_map/ppermute | solution.py:387
  4.9 14.5 %collective-permute-start.2 = (bf16[528,256]{1,0:T(8,128)(2,1)S(1)}, bf16[528,256]{1,0:T(8,128)(2,1)S(1)}, u32[]{:S(2)}, u32[]{:S(2)}) collective-permute-start(bf16[528,256]{1,0:T(8,128)(2,1)S(1)} %get-tuple-element.25.own_ref), channel_id=1, source_target_pairs={{0,2},{1,3},{2,4},{3,5},{4,6},{5,7},{6,8},{7,9},{8,10},{9,11},{10,... | collective-permute-start | bytes 811016 | tf_op jit(solution)/shard_map/ppermute | solution.py:387
  8.4 12.9 %collective-permute-start.4 = (bf16[528,256]{1,0:T(8,128)(2,1)S(1)}, bf16[528,256]{1,0:T(8,128)(2,1)S(1)}, u32[]{:S(2)}, u32[]{:S(2)}) collective-permute-start(bf16[528,256]{1,0:T(8,128)(2,1)S(1)} %get-tuple-element.25.own_ref), channel_id=1, source_target_pairs={{0,1},{2,3},{4,5},{6,7},{8,9},{10,11},{12,13},{14,15},{16,17},{18,... | collective-permute-start | bytes 811016 | tf_op jit(solution)/shard_map/ppermute | solution.py:387
  15.9 5.3 %collective-permute-start.5 = (bf16[528,256]{1,0:T(8,128)(2,1)S(1)}, bf16[528,256]{1,0:T(8,128)(2,1)S(1)}, u32[]{:S(2)}, u32[]{:S(2)}) collective-permute-start(bf16[528,256]{1,0:T(8,128)(2,1)S(1)} %collective-permute-done.refs_3_), channel_id=1, source_target_pairs={{0,1},{1,0},{2,3},{3,2},{4,5},{5,4},{6,7},{7,6},{8,9},{9,8},{10,11... | collective-permute-start | bytes 811016 | tf_op jit(solution)/shard_map/ppermute | solution.py:391
  16.0 48.4 %collective-permute-start.1 = (bf16[528,256]{1,0:T(8,128)(2,1)S(1)}, bf16[528,256]{1,0:T(8,128)(2,1)S(1)}, u32[]{:S(2)}, u32[]{:S(2)}) collective-permute-start(bf16[528,256]{1,0:T(8,128)(2,1)S(1)} %collective-permute-done.refs_3_), channel_id=1, source_target_pairs={{0,2},{1,3},{2,4},{3,5},{4,6},{5,7},{6,8},{7,9},{8,10},{9,11},{10,... | collective-permute-start | bytes 811016 | tf_op jit(solution)/shard_map/ppermute | solution.py:387
  19.5 45.0 %collective-permute-start.3 = (bf16[528,256]{1,0:T(8,128)(2,1)S(1)}, bf16[528,256]{1,0:T(8,128)(2,1)S(1)}, u32[]{:S(2)}, u32[]{:S(2)}) collective-permute-start(bf16[528,256]{1,0:T(8,128)(2,1)S(1)} %collective-permute-done.2.refs_5_), channel_id=1, source_target_pairs={{0,1},{1,0},{2,3},{3,2},{4,5},{5,4},{6,7},{7,6},{8,9},{9,8},{10,11... | collective-permute-start | bytes 811016 | tf_op jit(solution)/shard_map/ppermute | solution.py:391
  19.7 59.2 %collective-permute-start.7 = (bf16[528,256]{1,0:T(8,128)(2,1)S(1)}, bf16[528,256]{1,0:T(8,128)(2,1)S(1)}, u32[]{:S(2)}, u32[]{:S(2)}) collective-permute-start(bf16[528,256]{1,0:T(8,128)(2,1)S(1)} %collective-permute-done.refs_3_), channel_id=1, source_target_pairs={{1,4},{3,6},{5,8},{7,10},{9,12},{11,14},{17,20},{19,22},{21,24},{2... | collective-permute-start | bytes 811016 | tf_op jit(solution)/shard_map/ppermute | solution.py:387
  64.5 29.3 %collective-permute-start.6 = (bf16[528,256]{1,0:T(8,128)(2,1)S(1)}, bf16[528,256]{1,0:T(8,128)(2,1)S(1)}, u32[]{:S(2)}, u32[]{:S(2)}) collective-permute-start(bf16[528,256]{1,0:T(8,128)(2,1)S(1)} %collective-permute-done.1.refs_2_), channel_id=1, source_target_pairs={{0,1},{1,0},{2,3},{3,2},{4,5},{5,4},{6,7},{7,6},{8,9},{9,8},{10,11... | collective-permute-start | bytes 811016 | tf_op jit(solution)/shard_map/ppermute | solution.py:391
